TPU v7x, 32 devices: a whole 2x2x4 slice. The times are simulated.
32 devices in a mesh: row: 4 (over y, x), col: 8 (over z, core).
Axes of the slice: x: 2, y: 2, z: 4, core: 2. Of those that a mesh axis runs over, the one named last changes fastest.
Arguments:
- matrix: float32 [2, 4, 256, 1, 8, 256], P(None, 'row', None, None, 'col'), as said below
Outputs:
- factored: float32 [2, 4, 256, 1, 8, 256], P(None, 'row', None, None, 'col')
Inputs may be any that keep to these rules, and one draw needn't show every extreme that they name: `matrix`: symmetric and positive definite.
All inputs are finite; a program needn't handle non-finite values.
Results may differ from a plain program's by a relative error of at most 0.0001.
Values sent between devices are 32-bit elements; how exact they have to be, the bound alone decides.
A program may use at most 128 MiB of HBM per device.

v0:
```python
import functools

import jax
import jax.numpy as jnp
from jax import lax
from jax.experimental import pallas as pl
from jax.experimental.pallas import tpu as pltpu
from jax.sharding import PartitionSpec as P

STEPS = 8
LANES = 128
SUBS = 8
PANEL = 64
ROOT_COL = 2
MESH = pl.DeviceIdType.MESH
NT = (((1,), (1,)), ((), ()))
TN = (((0,), (0,)), ((), ()))


def split(value):
    high = value.astype(jnp.bfloat16)
    low = (value - high.astype(jnp.float32)).astype(jnp.bfloat16)
    return high, low


def dot3(a_high, a_low, b_high, b_low):
    def one(a, b):
        return lax.dot_general(a, b, NT, preferred_element_type=jnp.float32)

    return one(a_high, b_high) + (one(a_high, b_low) + one(a_low, b_high))


def factor_panel(work, width, base, start):
    groups = PANEL // SUBS
    chunks = (width + LANES) // LANES
    offset = start - base
    shape = (SUBS, LANES)
    sub = lax.broadcasted_iota(jnp.int32, shape, 0)
    rows = []
    for g in range(groups):
        at = pl.ds(pl.multiple_of(start + g * SUBS, SUBS), SUBS)
        row = [work[at, base + h * LANES : base + (h + 1) * LANES] for h in range(chunks)]
        row.append(pltpu.roll(row[0], lax.rem(LANES - offset, LANES), 1))
        rows.append(row)
    for b in range(groups):
        lane = b * SUBS
        cols = [
            [jnp.broadcast_to(rows[g][chunks][:, lane + t : lane + t + 1], shape) for g in range(b, groups)]
            for t in range(SUBS)
        ]
        scales = jnp.ones(shape, jnp.float32)
        for t in range(SUBS):
            scale = lax.rsqrt(jnp.broadcast_to(cols[t][0][t : t + 1, :], shape))
            scales = jnp.where(sub == t, scale, scales)
            mult = [c * scale for c in cols[t]]
            for r in range(t + 1, SUBS):
                across = jnp.broadcast_to(mult[0][r : r + 1, :], shape)
                cols[r] = [c - m * across for c, m in zip(cols[r], mult)]
            below = jnp.where(sub > t, mult[0], 0.0)
            for h in range(chunks + 1):
                pivot = jnp.broadcast_to(rows[b][h][t : t + 1, :], shape) * scale
                rows[b][h] = rows[b][h] - below * pivot
                for g in range(b + 1, groups):
                    rows[g][h] = rows[g][h] - mult[g - b] * pivot
        rows[b] = [r * scales for r in rows[b]]
    for g in range(groups):
        at = pl.ds(pl.multiple_of(start + g * SUBS, SUBS), SUBS)
        for h in range(chunks):
            work[at, base + h * LANES : base + (h + 1) * LANES] = rows[g][h]
    whole = jnp.concatenate([jnp.concatenate(row[:chunks], 1) for row in rows], 0)
    high, low = split(whole)
    rest = width - base
    left = whole[:, :rest]
    left = jnp.where(lax.broadcasted_iota(jnp.int32, left.shape, 1) >= offset + PANEL, left, 0.0)
    left_high, left_low = split(left)
    update = lax.dot_general(
        jnp.concatenate([left_high, left_high, left_low], 0),
        jnp.concatenate([high, low, high], 0),
        TN,
        preferred_element_type=jnp.float32,
    )
    work[base:width, base : base + width + LANES] -= update


def factor_tile(work, width):
    for base in range(0, width, LANES):
        def one(i, carry, base=base):
            factor_panel(work, width, base, base + i * PANEL)
            return carry

        lax.fori_loop(0, LANES // PANEL, one, 0)


def kernel(dims, x_ref, o_ref, tiles, high, low, work, inv_high, inv_low, in_sem, out_sem, send_sem, land_sem, go_sem):
    steps, num_row, num_col = dims
    row_tiles, width, _ = x_ref.shape
    my_row, my_col = lax.axis_index("row"), lax.axis_index("col")
    root_row, root_col = num_row - 1, min(ROOT_COL, num_col - 1)
    home = (root_row, root_col)
    root = jnp.logical_and(my_row == root_row, my_col == root_col)
    count = num_row * num_col
    barrier = pltpu.get_barrier_semaphore()

    def inbound(a, i, slot, device):
        return pltpu.make_async_remote_copy(
            src_ref=x_ref.at[a], dst_ref=tiles.at[slot], send_sem=send_sem.at[a], recv_sem=in_sem.at[slot],
            device_id=device, device_id_type=MESH,
        )

    def outbound(slot, a, device):
        return pltpu.make_async_remote_copy(
            src_ref=tiles.at[slot], dst_ref=o_ref.at[a], send_sem=out_sem.at[slot], recv_sem=land_sem.at[a],
            device_id=device, device_id_type=MESH,
        )

    beside = my_row == root_row
    ahead = jnp.where(jnp.logical_and(beside, my_col - 1 == root_col), my_col - 2, my_col - 1)
    after = jnp.where(jnp.logical_and(beside, my_col + 1 == root_col), my_col + 2, my_col + 1)
    follows, leads = ahead >= 0, after < num_col

    @pl.when(jnp.logical_not(root))
    def _():
        pl.semaphore_signal(barrier, inc=1, device_id=home, device_id_type=MESH)

        @pl.when(follows)
        def _():
            pl.semaphore_signal(barrier, inc=1, device_id=(my_row, ahead), device_id_type=MESH)

        pl.semaphore_wait(barrier, jnp.where(leads, 2, 1))

        @pl.when(follows)
        def _():
            pl.semaphore_wait(go_sem, 1)

        for a in range(row_tiles):
            i = a * num_row + my_row

            @pl.when(i >= my_col)
            def _():
                inbound(a, i, i * steps + my_col, home).start()

            @pl.when(i < my_col)
            def _():
                o_ref[a] = jnp.zeros((width, width), jnp.float32)

        for a in range(row_tiles):
            i = a * num_row + my_row

            @pl.when(i >= my_col)
            def _():
                inbound(a, i, i * steps + my_col, home).wait_send()

        @pl.when(leads)
        def _():
            pl.semaphore_signal(go_sem, inc=1, device_id=(my_row, after), device_id_type=MESH)

        for a in range(row_tiles):
            i = a * num_row + my_row

            @pl.when(i >= my_col)
            def _():
                outbound(0, a, home).wait_recv()

    @pl.when(root)
    def _():
        for a in range(row_tiles):
            i = a * num_row + root_row
            if i >= root_col:
                slot = i * steps + root_col
                pltpu.make_async_copy(x_ref.at[a], tiles.at[slot], in_sem.at[slot]).start()
            else:
                o_ref[a] = jnp.zeros((width, width), jnp.float32)

        def greet(d, carry):
            d = jnp.where(d >= root_row * num_col + root_col, d + 1, d)
            pl.semaphore_signal(
                barrier, inc=1, device_id=(d // num_col, lax.rem(d, num_col)), device_id_type=MESH
            )
            return carry

        lax.fori_loop(0, count - 1, greet, 0)
        pl.semaphore_wait(barrier, count - 1)

        def arrive(slot):
            pltpu.make_async_copy(tiles.at[slot], tiles.at[slot], in_sem.at[slot]).wait()

        def owned(i, k):
            return jnp.logical_and(lax.rem(i, num_row) == root_row, k == root_col)

        def send(i, k):
            slot = i * steps + k

            @pl.when(owned(i, k))
            def _():
                pltpu.make_async_copy(tiles.at[slot], o_ref.at[i // num_row], out_sem.at[slot]).start()

            @pl.when(jnp.logical_not(owned(i, k)))
            def _():
                outbound(slot, i // num_row, (lax.rem(i, num_row), k)).start()

        def block(i):
            return pl.ds(pl.multiple_of(i * width, width), width)

        def subtract(i, k):
            slot = i * steps + k
            arrive(slot)

            def one(m, carry):
                tiles[slot] -= dot3(
                    high[block(i), block(m)], low[block(i), block(m)],
                    high[block(k), block(m)], low[block(k), block(m)],
                )
                return carry

            lax.fori_loop(0, k, one, 0)

        def step(k, carry):
            slot = k * steps + k
            subtract(k, k)
            rows = lax.broadcasted_iota(jnp.int32, (width, width), 0)
            cols = lax.broadcasted_iota(jnp.int32, (width, width), 1)
            work[:, :width] = tiles[slot]
            work[:, width:] = jnp.where(rows == cols, 1.0, 0.0)
            factor_tile(work, width)
            tiles[slot] = jnp.where(cols >= rows, work[:, :width], 0.0).T
            inv_high[...], inv_low[...] = split(work[:, width:])

            def panel(i, carry):
                send(i - 1, k)
                subtract(i, k)
                spot = i * steps + k
                a_high, a_low = split(tiles[spot])
                solved = dot3(a_high, a_low, inv_high[...], inv_low[...])
                tiles[spot] = solved
                high[block(i), block(k)], low[block(i), block(k)] = split(solved)
                return carry

            lax.fori_loop(k + 1, steps, panel, 0)

            send(steps - 1, k)
            return carry

        lax.fori_loop(0, steps, step, 0)

        def finish(k, carry):
            def one(i, carry):
                slot = i * steps + k
                pltpu.make_async_copy(tiles.at[slot], tiles.at[slot], out_sem.at[slot]).wait()
                return carry

            return lax.fori_loop(k, steps, one, carry)

        lax.fori_loop(0, steps, finish, 0)


def on_root(matrix):
    row_tiles = matrix.shape[0]
    width = matrix.shape[2]
    num_row, num_col = lax.axis_size("row"), lax.axis_size("col")
    order = STEPS * width
    local = matrix.reshape(row_tiles, width, width)
    slots = STEPS * STEPS
    out = pl.pallas_call(
        functools.partial(kernel, (STEPS, num_row, num_col)),
        out_shape=jax.ShapeDtypeStruct(local.shape, jnp.float32),
        in_specs=[pl.BlockSpec(memory_space=pltpu.VMEM)],
        out_specs=pl.BlockSpec(memory_space=pltpu.VMEM),
        scratch_shapes=[
            pltpu.VMEM((slots, width, width), jnp.float32),
            pltpu.VMEM((order, order), jnp.bfloat16),
            pltpu.VMEM((order, order), jnp.bfloat16),
            pltpu.VMEM((width, 2 * width), jnp.float32),
            pltpu.VMEM((width, width), jnp.bfloat16),
            pltpu.VMEM((width, width), jnp.bfloat16),
            pltpu.SemaphoreType.DMA((slots,)),
            pltpu.SemaphoreType.DMA((slots,)),
            pltpu.SemaphoreType.DMA((row_tiles,)),
            pltpu.SemaphoreType.DMA((row_tiles,)),
            pltpu.SemaphoreType.REGULAR,
        ],
        compiler_params=pltpu.CompilerParams(collective_id=0, has_side_effects=True, vmem_limit_bytes=56 * 2**20),
    )(local)
    return out.reshape(matrix.shape)


def broadcast(value, axis, source):
    kept = jnp.where(lax.axis_index(axis) == source, value, 0).astype(value.dtype)
    return lax.psum(kept, axis)


def solve_panel(factor, column):
    width = column.shape[1]
    inverse = jax.scipy.linalg.solve_triangular(
        factor, jnp.eye(width, dtype=jnp.float32), lower=True
    )
    solved = jnp.einsum("ts,ars->art", inverse, column, precision=lax.Precision.HIGHEST)
    return solved


def stepwise(matrix):
    row_tiles = matrix.shape[0]
    width = matrix.shape[2]
    col_tiles = matrix.shape[3]
    tile_grid = matrix.reshape(row_tiles, width, col_tiles, width)
    num_row = lax.axis_size("row")
    num_col = lax.axis_size("col")
    my_row = lax.axis_index("row")
    my_col = lax.axis_index("col")
    rows_global = jnp.arange(row_tiles, dtype=jnp.int32) * num_row + my_row
    ratio = num_col // num_row
    for k in range(STEPS):
        lead_row = k % num_row
        lead_col = k % num_col
        local_row = k // num_row
        local_col = k // num_col
        column = tile_grid[:, :, local_col, :]
        candidate = tile_grid[local_row, :, local_col, :]
        keep = (rows_global > k)[:, None, None]
        diag_tile = broadcast(candidate, "row", lead_row)
        factor = jnp.linalg.cholesky(diag_tile)
        local_panel = jnp.where(keep, solve_panel(factor, column), 0.0)
        panel_rows = broadcast(local_panel, "col", lead_col)
        grouped = panel_rows.reshape(col_tiles, ratio, width, width)
        chosen = lax.dynamic_index_in_dim(grouped, my_col // num_row, 1, keepdims=False)
        panel_cols = broadcast(chosen, "row", my_col % num_row)
        update = jnp.einsum(
            "art,bst->arbs", panel_rows, panel_cols, precision=lax.Precision.HIGHEST
        )
        tile_grid = tile_grid - update
        diagonal_part = jnp.where((rows_global == k)[:, None, None], factor[None], 0.0)
        new_column = panel_rows + diagonal_part
        old_column = tile_grid[:, :, local_col, :]
        tile_grid = tile_grid.at[:, :, local_col, :].set(
            jnp.where(my_col == lead_col, new_column, old_column)
        )
    return tile_grid.reshape(matrix.shape)


def on_device(matrix):
    row_tiles, _, _, col_tiles = matrix.shape[:4]
    whole = row_tiles * lax.axis_size("row") == STEPS and lax.axis_size("col") == STEPS and col_tiles == 1
    return on_root(matrix) if whole else stepwise(matrix)


def solution(mesh):
    placed = (P(None, "row", None, None, "col", None),)
    return jax.shard_map(
        on_device,
        mesh=mesh,
        in_specs=placed,
        out_specs=P(None, "row", None, None, "col", None),
        check_vma=False,
    )
```

profile of v0, /device:TPU:31, one launch (start us, length us, event | category | flops | bytes accessed | tf_op | source)
XLA Modules:
  0.0 125.8 jit_solution(18196198617919452692)
XLA Ops:
  0.0 1.9 %copy.5 = f32[2,1,256,1,1,256]{5,2,3,4,1,0:T(8,128)} copy(f32[2,1,256,1,1,256]{5,4,3,2,1,0:T(1,128)} %param.1) | data formatting | bytes 1048576
  1.9 121.5 %shard_map.17 = f32[2,256,256]{2,1,0:T(8,128)} custom-call(f32[2,256,256]{2,1,0:T(8,128)} %bitcast.5), custom_call_target="tpu_custom_call" | custom-call | tf_op jit(solution)/shard_map/pallas_call | solution.py:263
  123.4 2.4 %copy.2 = f32[2,1,256,1,1,256]{5,4,3,2,1,0:T(1,128)} copy(f32[2,1,256,1,1,256]{5,2,0,4,3,1:T(8,128)} %bitcast.4) | data formatting | bytes 1048576 | tf_op jit(solution)/shard_map/reshape | solution.py:283
where the time goes:
time: 126 us
  Pallas kernels  122 us (97%)
  local copies, waits for them, and re-layouts  4.24 us (3%)
    pallas_call x1, Pallas kernels, on_root(): pl.pallas_call(functools.partial(kernel, (STEPS, num_row, num_col)), out_...  122 us

commit v1 on v0

--- a/solution.py
+++ b/solution.py
@@ -11,6 +11,8 @@
 LANES = 128
 SUBS = 8
 PANEL = 64
+BLOCK = 16
+SHAPE = (SUBS, LANES)
 ROOT_COL = 2
 MESH = pl.DeviceIdType.MESH
 NT = (((1,), (1,)), ((), ()))
@@ -30,68 +32,103 @@
     return one(a_high, b_high) + (one(a_high, b_low) + one(a_low, b_high))
 
 
-def factor_panel(work, width, base, start):
-    groups = PANEL // SUBS
-    chunks = (width + LANES) // LANES
-    offset = start - base
-    shape = (SUBS, LANES)
-    sub = lax.broadcasted_iota(jnp.int32, shape, 0)
-    rows = []
+def spread(value, at):
+    return jnp.broadcast_to(value[at:at+1,:], SHAPE)
+
+def factor_panel(work, diag, unit, width, start):
+    groups = PANEL//SUBS
+    chunks = width//LANES
+    sub = lax.broadcasted_iota(jnp.int32, SHAPE, 0)
+    lane = lax.broadcasted_iota(jnp.int32, SHAPE, 1)
+    rows = [[work[start+g*SUBS:start+(g+1)*SUBS, h*LANES:(h+1)*LANES] for h in range(chunks)] for g in range(groups)]
+    per = BLOCK//SUBS
+    for b in range(PANEL//BLOCK):
+        home = b*per
+        l0 = start + b*BLOCK
+        hc, off = l0//LANES, l0%LANES
+        def pick(g, t):
+            return jnp.take_along_axis(rows[g][hc], jnp.full(SHAPE, off+t, jnp.int32), axis=1)
+        near = min(home+2*per, groups)
+        far = list(range(near, groups))
+        cols = [{g: pick(g,t) for g in range(home + t//SUBS, near)} for t in range(BLOCK)]
+        fcols = [{g: pick(g,t) for g in far} for t in range(SUBS)] + [{}]*SUBS
+        scales = {g: jnp.ones(SHAPE, jnp.float32) for g in range(home, home+per)}
+        lower = {g: jnp.zeros(SHAPE, jnp.float32) for g in range(home, home+per)}
+        for t in range(0, BLOCK, 2):
+            top = home + t//SUBS
+            r = t%SUBS
+            if t == SUBS and far:
+                fcols = [None]*SUBS + [{g: pick(g,SUBS+q) for g in far} for q in range(SUBS)]
+            if r == 0:
+                inside = jnp.logical_and(lane>=off+t, lane<off+t+SUBS)
+                eye = jnp.where(lane == off+t+sub, unit[hc], 0.0)
+                for g in range(top, groups):
+                    rows[g][hc] = jnp.where(inside, eye if g == top else 0.0, rows[g][hc])
+            x, y = dict(cols[t]), dict(cols[t+1])
+            fx, fy = fcols[t], fcols[t+1]
+            a, bb, c = spread(x[top], r), spread(x[top], r+1), spread(y[top], r+1)
+            det = a*c - bb*bb
+            ra = lax.rsqrt(a)
+            rd = lax.rsqrt(a*det)
+            ia, iad = ra*ra, rd*rd
+            u = {g: y[g]*a - x[g]*bb for g in y}
+            fu = {g: fy[g]*a - fx[g]*bb for g in far}
+            mx = {g: x[g]*ia for g in x}
+            mu = {g: u[g]*iad for g in u}
+            fmx = {g: fx[g]*ia for g in far}
+            fmu = {g: fu[g]*iad for g in far}
+            for s in range(t+2, BLOCK):
+                gs, q = home + s//SUBS, s%SUBS
+                xs, us = spread(x[gs], q), spread(u[gs], q)
+                for g in cols[s]:
+                    if s < t+4 and g == gs:
+                        cols[s][g] = (cols[s][g] - xs*mx[g]) - (us*u[g])*iad
+                    else:
+                        cols[s][g] = cols[s][g] - xs*mx[g] - us*mu[g]
+                if s < SUBS or t >= SUBS:
+                    for g in far:
+                        fcols[s][g] = fcols[s][g] - xs*fmx[g] - us*fmu[g]
+            for g in [top]:
+                lower[g] = jnp.where(lane==off+t, x[g]*ra, jnp.where(lane==off+t+1, u[g]*rd, lower[g]))
+            scales[top] = jnp.where(sub==r, ra, jnp.where(sub==r+1, a*rd, scales[top]))
+            mx[top] = jnp.where(sub>r, mx[top], 0.0)
+            mu[top] = jnp.where(sub>r+1, mu[top], 0.0)
+            for h in range(chunks):
+                p0, q1 = spread(rows[top][h], r), spread(rows[top][h], r+1)
+                p1 = q1*a - p0*bb
+                for g in range(top, groups):
+                    m, n = (fmx[g], fmu[g]) if g in far else (mx[g], mu[g])
+                    rows[g][h] = rows[g][h] - m*p0 - n*p1
+            if r == SUBS-2:
+                rows[top] = [v*scales[top] for v in rows[top]]
+        for g in range(home, home+per):
+            diag[start+g*SUBS:start+(g+1)*SUBS, :] = lower[g]
     for g in range(groups):
-        at = pl.ds(pl.multiple_of(start + g * SUBS, SUBS), SUBS)
-        row = [work[at, base + h * LANES : base + (h + 1) * LANES] for h in range(chunks)]
-        row.append(pltpu.roll(row[0], lax.rem(LANES - offset, LANES), 1))
-        rows.append(row)
-    for b in range(groups):
-        lane = b * SUBS
-        cols = [
-            [jnp.broadcast_to(rows[g][chunks][:, lane + t : lane + t + 1], shape) for g in range(b, groups)]
-            for t in range(SUBS)
-        ]
-        scales = jnp.ones(shape, jnp.float32)
-        for t in range(SUBS):
-            scale = lax.rsqrt(jnp.broadcast_to(cols[t][0][t : t + 1, :], shape))
-            scales = jnp.where(sub == t, scale, scales)
-            mult = [c * scale for c in cols[t]]
-            for r in range(t + 1, SUBS):
-                across = jnp.broadcast_to(mult[0][r : r + 1, :], shape)
-                cols[r] = [c - m * across for c, m in zip(cols[r], mult)]
-            below = jnp.where(sub > t, mult[0], 0.0)
-            for h in range(chunks + 1):
-                pivot = jnp.broadcast_to(rows[b][h][t : t + 1, :], shape) * scale
-                rows[b][h] = rows[b][h] - below * pivot
-                for g in range(b + 1, groups):
-                    rows[g][h] = rows[g][h] - mult[g - b] * pivot
-        rows[b] = [r * scales for r in rows[b]]
+        for h in range(chunks):
+            work[start+g*SUBS:start+(g+1)*SUBS, h*LANES:(h+1)*LANES] = rows[g][h]
+    stop = start+PANEL
+    if stop == width: return
+    hc = start//LANES
     for g in range(groups):
-        at = pl.ds(pl.multiple_of(start + g * SUBS, SUBS), SUBS)
-        for h in range(chunks):
-            work[at, base + h * LANES : base + (h + 1) * LANES] = rows[g][h]
-    whole = jnp.concatenate([jnp.concatenate(row[:chunks], 1) for row in rows], 0)
+        gap = jnp.logical_and(lane>=start%LANES+(g+1)*SUBS, lane<start%LANES+PANEL)
+        rows[g][hc] = jnp.where(gap, 0.0, rows[g][hc])
+    whole = jnp.concatenate([jnp.concatenate(r,1) for r in rows],0)
     high, low = split(whole)
-    rest = width - base
-    left = whole[:, :rest]
-    left = jnp.where(lax.broadcasted_iota(jnp.int32, left.shape, 1) >= offset + PANEL, left, 0.0)
-    left_high, left_low = split(left)
-    update = lax.dot_general(
-        jnp.concatenate([left_high, left_high, left_low], 0),
-        jnp.concatenate([high, low, high], 0),
-        TN,
-        preferred_element_type=jnp.float32,
-    )
-    work[base:width, base : base + width + LANES] -= update
-
-
-def factor_tile(work, width):
-    for base in range(0, width, LANES):
-        def one(i, carry, base=base):
-            factor_panel(work, width, base, base + i * PANEL)
-            return carry
-
-        lax.fori_loop(0, LANES // PANEL, one, 0)
-
-
-def kernel(dims, x_ref, o_ref, tiles, high, low, work, inv_high, inv_low, in_sem, out_sem, send_sem, land_sem, go_sem):
+    base = stop//LANES*LANES
+    lh, ll = high[:, base:], low[:, base:]
+    update = lax.dot_general(jnp.concatenate([lh,lh,ll],0), jnp.concatenate([high,low,high],0), TN, preferred_element_type=jnp.float32)
+    lanes = lax.broadcasted_iota(jnp.int32, (width-stop, width), 1)
+    old = jnp.where(jnp.logical_and(lanes >= start, lanes < stop), 0.0, work[stop:, :])
+    work[stop:, :] = old - update[stop-base:, :]
+
+def factor_tile(work, diag, scale_row, width):
+    chunks = width//LANES
+    unit = [jnp.broadcast_to(scale_row[:, h*LANES:(h+1)*LANES], SHAPE) for h in range(chunks)]
+    for start in range(0, width, PANEL):
+        factor_panel(work, diag, unit, width, start)
+
+
+def kernel(dims, x_ref, o_ref, tiles, high, low, work, corner, inv_high, inv_low, in_sem, out_sem, send_sem, land_sem, go_sem):
     steps, num_row, num_col = dims
     row_tiles, width, _ = x_ref.shape
     my_row, my_col = lax.axis_index("row"), lax.axis_index("col")
@@ -219,11 +256,19 @@
             subtract(k, k)
             rows = lax.broadcasted_iota(jnp.int32, (width, width), 0)
             cols = lax.broadcasted_iota(jnp.int32, (width, width), 1)
-            work[:, :width] = tiles[slot]
-            work[:, width:] = jnp.where(rows == cols, 1.0, 0.0)
-            factor_tile(work, width)
-            tiles[slot] = jnp.where(cols >= rows, work[:, :width], 0.0).T
-            inv_high[...], inv_low[...] = split(work[:, width:])
+            tile = tiles[slot]
+            only = jnp.where(rows == cols, tile, 0.0)
+            along = jnp.sum(only, axis=0, keepdims=True)
+            down = jnp.sum(only, axis=1, keepdims=True)
+            scale_row, scale_col = lax.rsqrt(along), lax.rsqrt(down)
+            work[...] = tile * scale_row * scale_col
+            factor_tile(work, corner, scale_row, width)
+            done = work[...]
+            inv_high[...], inv_low[...] = split(jnp.where(cols <= rows, done, 0.0))
+            upper = jnp.where(cols // SUBS > rows // SUBS, done * (along * scale_row), 0.0)
+            wide = jnp.concatenate([corner[...]] * (width // LANES), 1)
+            near = jnp.logical_and(cols // SUBS == rows // SUBS, cols <= rows)
+            tiles[slot] = upper.T + jnp.where(near, wide * (down * scale_col), 0.0)
 
             def panel(i, carry):
                 send(i - 1, k)
@@ -269,7 +314,8 @@
             pltpu.VMEM((slots, width, width), jnp.float32),
             pltpu.VMEM((order, order), jnp.bfloat16),
             pltpu.VMEM((order, order), jnp.bfloat16),
-            pltpu.VMEM((width, 2 * width), jnp.float32),
+            pltpu.VMEM((width, width), jnp.float32),
+            pltpu.VMEM((width, LANES), jnp.float32),
             pltpu.VMEM((width, width), jnp.bfloat16),
             pltpu.VMEM((width, width), jnp.bfloat16),
             pltpu.SemaphoreType.DMA((slots,)),

time: 126 us -> 104 us (0.83)
  Pallas kernels: 122 us -> 99.2 us
    pallas_call x1, Pallas kernels: 122 us -> 99.2 us  [on_root(): pl.pallas_call(functools.partial(kernel, (STEPS, num_row, num_col)), out_...]
where the time goes in v1:
time: 104 us; the launch traced here: 103 us
  Pallas kernels  99.2 us (95%)
  local copies, waits for them, and re-layouts  4.24 us (4%)
    pallas_call x1, Pallas kernels, on_root(): pl.pallas_call(functools.partial(kernel, (STEPS, num_row, num_col)), out_...  99.2 us
    reshape x1, local copies, waits for them, and re-layouts, on_root(): return out.reshape(matrix.shape)  2.37 us

profile of v1, /device:TPU:31, one launch (start us, length us, event | category | flops | bytes accessed | tf_op | source)
XLA Modules:
  0.0 103.4 jit_solution(9094310351080577174)
XLA Ops:
  0.0 1.9 %copy.5 = f32[2,1,256,1,1,256]{5,2,3,4,1,0:T(8,128)} copy(f32[2,1,256,1,1,256]{5,4,3,2,1,0:T(1,128)} %param.1) | data formatting | bytes 1048576
  1.9 99.2 %shard_map.17 = f32[2,256,256]{2,1,0:T(8,128)} custom-call(f32[2,256,256]{2,1,0:T(8,128)} %bitcast.5), custom_call_target="tpu_custom_call" | custom-call | tf_op jit(solution)/shard_map/pallas_call | solution.py:308
  101.0 2.4 %copy.2 = f32[2,1,256,1,1,256]{5,4,3,2,1,0:T(1,128)} copy(f32[2,1,256,1,1,256]{5,2,0,4,3,1:T(8,128)} %bitcast.4) | data formatting | bytes 1048576 | tf_op jit(solution)/shard_map/reshape | solution.py:329

commit v2 on v1

--- a/solution.py
+++ b/solution.py
@@ -13,7 +13,6 @@
 PANEL = 64
 BLOCK = 16
 SHAPE = (SUBS, LANES)
-ROOT_COL = 2
 MESH = pl.DeviceIdType.MESH
 NT = (((1,), (1,)), ((), ()))
 TN = (((0,), (0,)), ((), ()))
@@ -128,174 +127,364 @@
         factor_panel(work, diag, unit, width, start)
 
 
-def kernel(dims, x_ref, o_ref, tiles, high, low, work, corner, inv_high, inv_low, in_sem, out_sem, send_sem, land_sem, go_sem):
+def load(ref):
+    half = ref.shape[0] // 2
+    return jnp.concatenate([ref[pl.ds(h, half, stride=2), :] for h in range(2)], 1)
+
+
+def store(ref, value):
+    half = ref.shape[0] // 2
+    for h in range(2):
+        ref[pl.ds(h, half, stride=2), :] = value[:, h * LANES : (h + 1) * LANES]
+
+
+def kernel(
+    dims, x_ref, o_ref, tiles, inverse, beside, relay, high, low, own_high, own_low, inv_high, inv_low, work, corner,
+    in_sem, out_sem, pass_sem, inv_in, inv_out, first_out, side_in, side_out, send_sem, land_sem, relay_in, relay_out,
+    go_sem,
+):
     steps, num_row, num_col = dims
-    row_tiles, width, _ = x_ref.shape
+    row_tiles = x_ref.shape[0]
+    width = work.shape[0]
     my_row, my_col = lax.axis_index("row"), lax.axis_index("col")
-    root_row, root_col = num_row - 1, min(ROOT_COL, num_col - 1)
-    home = (root_row, root_col)
-    root = jnp.logical_and(my_row == root_row, my_col == root_col)
+    root_row = num_row - 1
+    chief, helper = (root_row, 3), (root_row, 2)
+    first = jnp.logical_and(my_row == 0, my_col == 0)
+    is_chief = jnp.logical_and(my_row == chief[0], my_col == chief[1])
+    is_helper = jnp.logical_and(my_row == helper[0], my_col == helper[1])
     count = num_row * num_col
+    me = my_row * num_col + my_col
     barrier = pltpu.get_barrier_semaphore()
-
-    def inbound(a, i, slot, device):
+    far = jnp.logical_or(my_col < 2, my_col > 3)
+
+    def remote(src, dst, send, recv, device):
         return pltpu.make_async_remote_copy(
-            src_ref=x_ref.at[a], dst_ref=tiles.at[slot], send_sem=send_sem.at[a], recv_sem=in_sem.at[slot],
-            device_id=device, device_id_type=MESH,
+            src_ref=src, dst_ref=dst, send_sem=send, recv_sem=recv, device_id=device, device_id_type=MESH
         )
 
-    def outbound(slot, a, device):
-        return pltpu.make_async_remote_copy(
-            src_ref=tiles.at[slot], dst_ref=o_ref.at[a], send_sem=out_sem.at[slot], recv_sem=land_sem.at[a],
-            device_id=device, device_id_type=MESH,
-        )
-
-    beside = my_row == root_row
-    ahead = jnp.where(jnp.logical_and(beside, my_col - 1 == root_col), my_col - 2, my_col - 1)
-    after = jnp.where(jnp.logical_and(beside, my_col + 1 == root_col), my_col + 2, my_col + 1)
-    follows, leads = ahead >= 0, after < num_col
-
-    @pl.when(jnp.logical_not(root))
-    def _():
-        pl.semaphore_signal(barrier, inc=1, device_id=home, device_id_type=MESH)
-
-        @pl.when(follows)
+    def local(src, dst, sem):
+        return pltpu.make_async_copy(src, dst, sem)
+
+    def settle(ref, sem):
+        pltpu.make_async_copy(ref, ref, sem).wait()
+
+    def own(a):
+        return (a * num_row + my_row) * steps + my_col
+
+    def to_chief(a):
+        return remote(x_ref.at[a], tiles.at[own(a)], send_sem.at[a], in_sem.at[own(a)], chief)
+
+    def to_helper(a):
+        return remote(x_ref.at[a], tiles.at[own(a)], send_sem.at[a], in_sem.at[own(a)], helper)
+
+    def to_relay(a):
+        return remote(x_ref.at[a], relay.at[my_row], send_sem.at[a], relay_in.at[my_row], (root_row, my_col))
+
+    def onward(p):
+        slot = (num_row + p) * steps + my_col
+        return remote(relay.at[p], tiles.at[slot], relay_out.at[p], in_sem.at[slot], helper)
+
+    def signal(sem, device):
+        pl.semaphore_signal(sem, inc=1, device_id=device, device_id_type=MESH)
+
+    relayed = jnp.logical_and(far, jnp.logical_and(my_row < 2, num_row + my_row >= my_col))
+    relays = [
+        jnp.logical_and(jnp.logical_and(my_row == root_row, far), num_row + p >= my_col) for p in range(2)
+    ]
+
+    @pl.when(jnp.logical_not(is_chief))
+    def _():
+        signal(barrier, chief)
+
+    @pl.when(jnp.logical_not(is_helper))
+    def _():
+        signal(barrier, helper)
+
+    for p in range(2):
+
+        @pl.when(relays[p])
+        def _(p=p):
+            signal(barrier, (p, my_col))
+
+    @pl.when(jnp.logical_or(is_chief, is_helper))
+    def _():
+        def greet(d, carry):
+            signal(barrier, (d // num_col, lax.rem(d, num_col)))
+            return carry
+
+        mine = chief[0] * num_col + jnp.where(is_chief, chief[1], helper[1])
+        other = chief[0] * num_col + jnp.where(is_chief, helper[1], chief[1])
+        low_end, high_end = jnp.minimum(mine, other), jnp.maximum(mine, other)
+        lax.fori_loop(0, low_end, greet, 0)
+        lax.fori_loop(high_end + 1, count, greet, 0)
+        pl.semaphore_wait(barrier, count - 1)
+
+    @pl.when(jnp.logical_not(jnp.logical_or(first, jnp.logical_or(is_chief, is_helper))))
+    def _():
+        pl.semaphore_wait(barrier, jnp.where(relayed, 3, 2))
+
+    for a in range(row_tiles):
+
+        @pl.when(a * num_row + my_row < my_col)
+        def _(a=a):
+            o_ref[a] = jnp.zeros(o_ref.shape[1:], jnp.float32)
+
+    begin = jnp.logical_and(my_row == 1, my_col <= 1)
+
+    @pl.when(begin)
+    def _():
+        to_chief(0).start()
+
+    early = jnp.logical_and(jnp.logical_and(my_row >= 2, my_row >= my_col), jnp.logical_not(is_helper))
+
+    @pl.when(early)
+    def _():
+        to_helper(0).start()
+
+    @pl.when(is_helper)
+    def _():
+        for a in range(row_tiles):
+            local(x_ref.at[a], tiles.at[own(a)], in_sem.at[own(a)]).start()
+
+    @pl.when(jnp.logical_and(relayed, jnp.logical_not(first)))
+    def _():
+        to_relay(1).start()
+
+    for p in range(2):
+
+        @pl.when(relays[p])
+        def _(p=p):
+            settle(relay.at[p], relay_in.at[p])
+            onward(p).start()
+
+    last = num_row + my_row >= my_col
+    late = jnp.logical_and(
+        last, jnp.logical_or(my_row == 2, jnp.logical_and(my_row < 2, jnp.logical_not(far)))
+    )
+
+    @pl.when(late)
+    def _():
+        pl.semaphore_wait(go_sem, 1)
+
+    end = jnp.logical_or(late, jnp.logical_and(my_row == root_row, jnp.logical_not(is_helper)))
+
+    @pl.when(end)
+    def _():
+        to_helper(1).start()
+
+    def arrive(slot):
+        settle(tiles.at[slot], in_sem.at[slot])
+
+    def deliver(slot, a, row, col):
+        return remote(tiles.at[slot], o_ref.at[a], out_sem.at[slot], land_sem.at[a], (row, col))
+
+    def send(i, k):
+        slot = i * steps + k
+        row, a = lax.rem(i, num_row), i // num_row
+        home = jnp.logical_and(my_row == row, my_col == k)
+
+        @pl.when(home)
         def _():
-            pl.semaphore_signal(barrier, inc=1, device_id=(my_row, ahead), device_id_type=MESH)
-
-        pl.semaphore_wait(barrier, jnp.where(leads, 2, 1))
-
-        @pl.when(follows)
+            local(tiles.at[slot], o_ref.at[a], out_sem.at[slot]).start()
+
+        @pl.when(jnp.logical_not(home))
         def _():
-            pl.semaphore_wait(go_sem, 1)
-
-        for a in range(row_tiles):
-            i = a * num_row + my_row
-
-            @pl.when(i >= my_col)
-            def _():
-                inbound(a, i, i * steps + my_col, home).start()
-
-            @pl.when(i < my_col)
-            def _():
-                o_ref[a] = jnp.zeros((width, width), jnp.float32)
-
-        for a in range(row_tiles):
-            i = a * num_row + my_row
-
-            @pl.when(i >= my_col)
-            def _():
-                inbound(a, i, i * steps + my_col, home).wait_send()
-
-        @pl.when(leads)
-        def _():
-            pl.semaphore_signal(go_sem, inc=1, device_id=(my_row, after), device_id_type=MESH)
-
-        for a in range(row_tiles):
-            i = a * num_row + my_row
-
-            @pl.when(i >= my_col)
-            def _():
-                outbound(0, a, home).wait_recv()
-
-    @pl.when(root)
-    def _():
-        for a in range(row_tiles):
-            i = a * num_row + root_row
-            if i >= root_col:
-                slot = i * steps + root_col
-                pltpu.make_async_copy(x_ref.at[a], tiles.at[slot], in_sem.at[slot]).start()
-            else:
-                o_ref[a] = jnp.zeros((width, width), jnp.float32)
-
-        def greet(d, carry):
-            d = jnp.where(d >= root_row * num_col + root_col, d + 1, d)
-            pl.semaphore_signal(
-                barrier, inc=1, device_id=(d // num_col, lax.rem(d, num_col)), device_id_type=MESH
-            )
-            return carry
-
-        lax.fori_loop(0, count - 1, greet, 0)
-        pl.semaphore_wait(barrier, count - 1)
-
-        def arrive(slot):
-            pltpu.make_async_copy(tiles.at[slot], tiles.at[slot], in_sem.at[slot]).wait()
-
-        def owned(i, k):
-            return jnp.logical_and(lax.rem(i, num_row) == root_row, k == root_col)
-
-        def send(i, k):
-            slot = i * steps + k
-
-            @pl.when(owned(i, k))
-            def _():
-                pltpu.make_async_copy(tiles.at[slot], o_ref.at[i // num_row], out_sem.at[slot]).start()
-
-            @pl.when(jnp.logical_not(owned(i, k)))
-            def _():
-                outbound(slot, i // num_row, (lax.rem(i, num_row), k)).start()
-
-        def block(i):
-            return pl.ds(pl.multiple_of(i * width, width), width)
-
-        def subtract(i, k):
-            slot = i * steps + k
-            arrive(slot)
-
-            def one(m, carry):
-                tiles[slot] -= dot3(
-                    high[block(i), block(m)], low[block(i), block(m)],
-                    high[block(k), block(m)], low[block(k), block(m)],
-                )
-                return carry
-
-            lax.fori_loop(0, k, one, 0)
-
+            deliver(slot, a, row, k).start()
+
+    def inv_copy(k, sem, device):
+        return remote(inverse.at[k], inverse.at[k], sem, inv_in.at[k], device)
+
+    def side_copy(k):
+        return remote(tiles.at[(k + 1) * steps + k], beside.at[k], side_out.at[k], side_in.at[k], helper)
+
+    @pl.when(first)
+    def _():
+        local(x_ref.at[0], tiles.at[0], in_sem.at[0]).start()
+
+    @pl.when(jnp.logical_or(first, is_chief))
+    def _():
         def step(k, carry):
             slot = k * steps + k
-            subtract(k, k)
+
+            @pl.when(is_chief)
+            def _():
+                @pl.when(k == 1)
+                def _():
+                    settle(inverse.at[0], inv_in.at[0])
+                    inv_high[0], inv_low[0] = split(load(inverse.at[0]))
+
+                left = slot - 1
+                arrive(left)
+                a_high, a_low = split(load(tiles.at[left]))
+                solved = dot3(a_high, a_low, inv_high[0], inv_low[0])
+                store(tiles.at[left], solved)
+                own_high[...], own_low[...] = split(solved)
+
+                @pl.when(k < steps - 1)
+                def _():
+                    side_copy(k - 1).start()
+
+                send(k, k - 1)
+
+            arrive(slot)
+
+            @pl.when(k == 1)
+            def _():
+                for p in range(2):
+                    for q in range(2, 4):
+                        signal(go_sem, (p, q))
+
+            work[...] = load(tiles.at[slot])
+
+            @pl.when(is_chief)
+            def _():
+                work[...] -= dot3(own_high[...], own_low[...], own_high[...], own_low[...])
+
             rows = lax.broadcasted_iota(jnp.int32, (width, width), 0)
             cols = lax.broadcasted_iota(jnp.int32, (width, width), 1)
-            tile = tiles[slot]
+            tile = work[...]
             only = jnp.where(rows == cols, tile, 0.0)
             along = jnp.sum(only, axis=0, keepdims=True)
             down = jnp.sum(only, axis=1, keepdims=True)
             scale_row, scale_col = lax.rsqrt(along), lax.rsqrt(down)
             work[...] = tile * scale_row * scale_col
             factor_tile(work, corner, scale_row, width)
-            done = work[...]
-            inv_high[...], inv_low[...] = split(jnp.where(cols <= rows, done, 0.0))
-            upper = jnp.where(cols // SUBS > rows // SUBS, done * (along * scale_row), 0.0)
+
+            @pl.when(k < steps - 1)
+            def _():
+                found = jnp.where(cols <= rows, work[...], 0.0)
+                store(inverse.at[k], found)
+                inv_high[0], inv_low[0] = split(found)
+
+            @pl.when(first)
+            def _():
+                pl.semaphore_wait(barrier, 3)
+                inv_copy(k, first_out.at[0], chief).start()
+                inv_copy(k, first_out.at[1], helper).start()
+
+            @pl.when(jnp.logical_and(is_chief, k < steps - 2))
+            def _():
+                inv_copy(k, inv_out.at[k], helper).start()
+
+            upper = jnp.where(cols // SUBS > rows // SUBS, work[...] * (along * scale_row), 0.0)
             wide = jnp.concatenate([corner[...]] * (width // LANES), 1)
             near = jnp.logical_and(cols // SUBS == rows // SUBS, cols <= rows)
-            tiles[slot] = upper.T + jnp.where(near, wide * (down * scale_col), 0.0)
-
-            def panel(i, carry):
-                send(i - 1, k)
-                subtract(i, k)
+            store(tiles.at[slot], upper.T + jnp.where(near, wide * (down * scale_col), 0.0))
+            send(k, k)
+            return carry
+
+        lax.fori_loop(jnp.where(first, 0, 1), jnp.where(first, 1, steps), step, 0)
+
+    @pl.when(first)
+    def _():
+        to_relay(1).start()
+        settle(tiles.at[0], out_sem.at[0])
+        inv_copy(0, first_out.at[0], chief).wait_send()
+        inv_copy(0, first_out.at[1], helper).wait_send()
+
+    @pl.when(is_chief)
+    def _():
+        def finish(k, carry):
+            settle(tiles.at[k * steps + k], out_sem.at[k * steps + k])
+            settle(tiles.at[k * steps + k - 1], out_sem.at[k * steps + k - 1])
+
+            @pl.when(k < steps - 1)
+            def _():
+                settle(beside.at[k - 1], side_out.at[k - 1])
+
+            @pl.when(k < steps - 2)
+            def _():
+                settle(inverse.at[k], inv_out.at[k])
+
+            return carry
+
+        lax.fori_loop(1, steps, finish, 0)
+
+    def block(i):
+        return pl.ds(pl.multiple_of(i * width, width), width)
+
+    @pl.when(is_helper)
+    def _():
+        def row(i, carry):
+            def whole(j, carry):
+                arrive(i * steps + j)
+                return carry
+
+            lax.fori_loop(0, i + 1, whole, 0)
+
+            @pl.when(i == 2)
+            def _():
+                for q in range(num_col - 1):
+                    signal(go_sem, (2, q))
+
+            def stage(k, carry):
+                @pl.when(k == i - 2)
+                def _():
+                    settle(inverse.at[k], inv_in.at[k])
+                    inv_high[k], inv_low[k] = split(load(inverse.at[k]))
+                    settle(beside.at[k], side_in.at[k])
+                    high[block(k + 1), block(k)], low[block(k + 1), block(k)] = split(load(beside.at[k]))
+
                 spot = i * steps + k
-                a_high, a_low = split(tiles[spot])
-                solved = dot3(a_high, a_low, inv_high[...], inv_low[...])
-                tiles[spot] = solved
+                a_high, a_low = split(load(tiles.at[spot]))
+                solved = dot3(a_high, a_low, inv_high[k], inv_low[k])
+                store(tiles.at[spot], solved)
                 high[block(i), block(k)], low[block(i), block(k)] = split(solved)
+                send(i, k)
+
+                def one(j, carry):
+                    slot = i * steps + j
+                    update = dot3(
+                        high[block(i), block(k)], low[block(i), block(k)],
+                        high[block(j), block(k)], low[block(j), block(k)],
+                    )
+                    store(tiles.at[slot], load(tiles.at[slot]) - update)
+                    return carry
+
+                lax.fori_loop(k + 1, i + 1, one, 0)
                 return carry
 
-            lax.fori_loop(k + 1, steps, panel, 0)
-
-            send(steps - 1, k)
+            lax.fori_loop(0, i - 1, stage, 0)
+            for j in (i - 1, i):
+                slot = i * steps + j
+                remote(tiles.at[slot], tiles.at[slot], pass_sem.at[slot], in_sem.at[slot], chief).start()
             return carry
 
-        lax.fori_loop(0, steps, step, 0)
-
-        def finish(k, carry):
-            def one(i, carry):
-                slot = i * steps + k
-                pltpu.make_async_copy(tiles.at[slot], tiles.at[slot], out_sem.at[slot]).wait()
+        lax.fori_loop(2, steps, row, 0)
+
+        def finish(i, carry):
+            def each(k, carry):
+                settle(tiles.at[i * steps + k], out_sem.at[i * steps + k])
                 return carry
 
-            return lax.fori_loop(k, steps, one, carry)
-
-        lax.fori_loop(0, steps, finish, 0)
+            lax.fori_loop(0, i - 1, each, 0)
+            for j in (i - 1, i):
+                settle(tiles.at[i * steps + j], pass_sem.at[i * steps + j])
+            return carry
+
+        lax.fori_loop(2, steps, finish, 0)
+
+    sent = [jnp.logical_or(begin, early), jnp.logical_or(relayed, end)]
+    for a in range(row_tiles):
+
+        @pl.when(sent[a])
+        def _(a=a):
+            to_helper(a).wait_send()
+
+        i = a * num_row + my_row
+        diagonal = jnp.logical_and(is_chief, i == my_col)
+        below = jnp.logical_and(is_helper, i >= my_col + 2)
+        mine = jnp.logical_or(jnp.logical_or(below, diagonal), jnp.logical_and(first, a == 0))
+
+        @pl.when(jnp.logical_and(i >= my_col, jnp.logical_not(mine)))
+        def _(a=a):
+            settle(o_ref.at[a], land_sem.at[a])
+
+    for p in range(2):
+
+        @pl.when(relays[p])
+        def _(p=p):
+            onward(p).wait_send()
 
 
 def on_root(matrix):
@@ -303,25 +492,30 @@
     width = matrix.shape[2]
     num_row, num_col = lax.axis_size("row"), lax.axis_size("col")
     order = STEPS * width
-    local = matrix.reshape(row_tiles, width, width)
+    tall = width * width // LANES
+    local = matrix.reshape(row_tiles, tall, LANES)
     slots = STEPS * STEPS
+    sem = pltpu.SemaphoreType.DMA
     out = pl.pallas_call(
         functools.partial(kernel, (STEPS, num_row, num_col)),
         out_shape=jax.ShapeDtypeStruct(local.shape, jnp.float32),
         in_specs=[pl.BlockSpec(memory_space=pltpu.VMEM)],
         out_specs=pl.BlockSpec(memory_space=pltpu.VMEM),
         scratch_shapes=[
-            pltpu.VMEM((slots, width, width), jnp.float32),
+            pltpu.VMEM((slots, tall, LANES), jnp.float32),
+            pltpu.VMEM((STEPS, tall, LANES), jnp.float32),
+            pltpu.VMEM((STEPS, tall, LANES), jnp.float32),
+            pltpu.VMEM((2, tall, LANES), jnp.float32),
             pltpu.VMEM((order, order), jnp.bfloat16),
             pltpu.VMEM((order, order), jnp.bfloat16),
+            pltpu.VMEM((width, width), jnp.bfloat16),
+            pltpu.VMEM((width, width), jnp.bfloat16),
+            pltpu.VMEM((STEPS, width, width), jnp.bfloat16),
+            pltpu.VMEM((STEPS, width, width), jnp.bfloat16),
             pltpu.VMEM((width, width), jnp.float32),
             pltpu.VMEM((width, LANES), jnp.float32),
-            pltpu.VMEM((width, width), jnp.bfloat16),
-            pltpu.VMEM((width, width), jnp.bfloat16),
-            pltpu.SemaphoreType.DMA((slots,)),
-            pltpu.SemaphoreType.DMA((slots,)),
-            pltpu.SemaphoreType.DMA((row_tiles,)),
-            pltpu.SemaphoreType.DMA((row_tiles,)),
+            sem((slots,)), sem((slots,)), sem((slots,)), sem((STEPS,)), sem((STEPS,)), sem((2,)), sem((STEPS,)),
+            sem((STEPS,)), sem((row_tiles,)), sem((row_tiles,)), sem((2,)), sem((2,)),
             pltpu.SemaphoreType.REGULAR,
         ],
         compiler_params=pltpu.CompilerParams(collective_id=0, has_side_effects=True, vmem_limit_bytes=56 * 2**20),
@@ -384,7 +578,7 @@
 
 def on_device(matrix):
     row_tiles, _, _, col_tiles = matrix.shape[:4]
-    whole = row_tiles * lax.axis_size("row") == STEPS and lax.axis_size("col") == STEPS and col_tiles == 1
+    whole = row_tiles == 2 and 2 * lax.axis_size("row") == STEPS and lax.axis_size("col") == STEPS and col_tiles == 1
     return on_root(matrix) if whole else stepwise(matrix)
 
 

time: 104 us -> 73.3 us (0.70)
  Pallas kernels: 99.2 us -> 70.9 us
  local copies, waits for them, and re-layouts: 4.24 us -> 2.19 us
    pallas_call x1, Pallas kernels: 99.2 us -> 70.9 us  [on_root(): pl.pallas_call(functools.partial(kernel, (STEPS, num_row, num_col)), out_...]
    reshape x1 -> x0, local copies, waits for them, and re-layouts: 2.37 us -> none  [on_root(): return out.reshape(matrix.shape)]
where the time goes in v2:
time: 73.3 us; the launch traced here: 73.1 us
  Pallas kernels  70.9 us (97%)
  local copies, waits for them, and re-layouts  2.19 us (3%)
    pallas_call x1, Pallas kernels, on_root(): pl.pallas_call(functools.partial(kernel, (STEPS, num_row, num_col)), out_...  70.9 us
    unnamed x1, local copies, waits for them, and re-layouts  2.19 us

profile of v2, /device:TPU:31, one launch (start us, length us, event | category | flops | bytes accessed | tf_op | source)
XLA Modules:
  0.0 73.1 jit_solution(7054910165968347855)
XLA Ops:
  0.0 70.9 %shard_map.17 = f32[2,512,128]{2,1,0:T(8,128)} custom-call(f32[2,512,128]{2,1,0:T(8,128)} %bitcast.3), custom_call_target="tpu_custom_call" | custom-call | tf_op jit(solution)/shard_map/pallas_call | solution.py:499
  70.9 2.2 %copy.4 = f32[2,1,256,1,1,256]{5,4,3,2,1,0:T(1,128)} copy(f32[2,1,256,1,1,256]{5,4,3,2,1,0:T(1,128)} %bitcast.2) | data formatting | bytes 1048576

commit v3 on v2

--- a/solution.py
+++ b/solution.py
@@ -14,6 +14,7 @@
 BLOCK = 16
 SHAPE = (SUBS, LANES)
 MESH = pl.DeviceIdType.MESH
+PASSED = ((4, 0), (4, 1), (4, 4), (5, 4), (5, 5), (6, 5), (6, 6))
 NT = (((1,), (1,)), ((), ()))
 TN = (((0,), (0,)), ((), ()))
 
@@ -34,7 +35,7 @@
 def spread(value, at):
     return jnp.broadcast_to(value[at:at+1,:], SHAPE)
 
-def factor_panel(work, diag, unit, width, start):
+def factor_panel(work, diag, unit, width, start, after):
     groups = PANEL//SUBS
     chunks = width//LANES
     sub = lax.broadcasted_iota(jnp.int32, SHAPE, 0)
@@ -106,6 +107,7 @@
         for h in range(chunks):
             work[start+g*SUBS:start+(g+1)*SUBS, h*LANES:(h+1)*LANES] = rows[g][h]
     stop = start+PANEL
+    after(start)
     if stop == width: return
     hc = start//LANES
     for g in range(groups):
@@ -120,11 +122,11 @@
     old = jnp.where(jnp.logical_and(lanes >= start, lanes < stop), 0.0, work[stop:, :])
     work[stop:, :] = old - update[stop-base:, :]
 
-def factor_tile(work, diag, scale_row, width):
+def factor_tile(work, diag, scale_row, width, after=lambda start: None):
     chunks = width//LANES
     unit = [jnp.broadcast_to(scale_row[:, h*LANES:(h+1)*LANES], SHAPE) for h in range(chunks)]
     for start in range(0, width, PANEL):
-        factor_panel(work, diag, unit, width, start)
+        factor_panel(work, diag, unit, width, start, after)
 
 
 def load(ref):
@@ -140,8 +142,8 @@
 
 def kernel(
     dims, x_ref, o_ref, tiles, inverse, beside, relay, high, low, own_high, own_low, inv_high, inv_low, work, corner,
-    in_sem, out_sem, pass_sem, inv_in, inv_out, first_out, side_in, side_out, send_sem, land_sem, relay_in, relay_out,
-    go_sem,
+    in_sem, out_sem, pass_sem, inv_in, inv_out, first_in, first_out, side_in, side_out, send_sem, land_sem, relay_in, relay_out,
+    half_sem, go_sem,
 ):
     steps, num_row, num_col = dims
     row_tiles = x_ref.shape[0]
@@ -187,10 +189,17 @@
     def signal(sem, device):
         pl.semaphore_signal(sem, inc=1, device_id=device, device_id_type=MESH)
 
-    relayed = jnp.logical_and(far, jnp.logical_and(my_row < 2, num_row + my_row >= my_col))
-    relays = [
-        jnp.logical_and(jnp.logical_and(my_row == root_row, far), num_row + p >= my_col) for p in range(2)
-    ]
+    def via(i, j):
+        return max(i % num_row, 1), 2 + j % 2
+
+    def at(row, col):
+        return jnp.logical_and(my_row == row, my_col == col)
+
+    second = num_row + my_row >= my_col
+    relayed = jnp.logical_and(jnp.logical_and(far, second), my_row < jnp.where(my_col > 3, 3, 2))
+    at_relay = jnp.logical_and(my_row == root_row, far)
+    relays = [jnp.logical_and(at_relay, num_row + p >= my_col) for p in range(2)]
+    relays.append(jnp.logical_and(at_relay, jnp.logical_and(my_col > 3, num_row + 2 >= my_col)))
 
     @pl.when(jnp.logical_not(is_chief))
     def _():
@@ -200,40 +209,76 @@
     def _():
         signal(barrier, helper)
 
-    for p in range(2):
+    for p in range(3):
 
         @pl.when(relays[p])
         def _(p=p):
             signal(barrier, (p, my_col))
 
+    for i, j in PASSED:
+
+        @pl.when(at(i % num_row, j))
+        def _(i=i, j=j):
+            signal(barrier, via(i, j))
+
+    @pl.when(at(0, 1))
+    def _():
+        signal(barrier, (root_row, 1))
+
     @pl.when(jnp.logical_or(is_chief, is_helper))
     def _():
         def greet(d, carry):
-            signal(barrier, (d // num_col, lax.rem(d, num_col)))
+            signal(barrier, (lax.rem(d, num_row), d // num_row))
             return carry
 
-        mine = chief[0] * num_col + jnp.where(is_chief, chief[1], helper[1])
-        other = chief[0] * num_col + jnp.where(is_chief, helper[1], chief[1])
-        low_end, high_end = jnp.minimum(mine, other), jnp.maximum(mine, other)
+        low_end, high_end = helper[1] * num_row + helper[0], chief[1] * num_row + chief[0]
         lax.fori_loop(0, low_end, greet, 0)
+        lax.fori_loop(low_end + 1, high_end, greet, 0)
         lax.fori_loop(high_end + 1, count, greet, 0)
         pl.semaphore_wait(barrier, count - 1)
 
     @pl.when(jnp.logical_not(jnp.logical_or(first, jnp.logical_or(is_chief, is_helper))))
     def _():
-        pl.semaphore_wait(barrier, jnp.where(relayed, 3, 2))
-
-    for a in range(row_tiles):
-
-        @pl.when(a * num_row + my_row < my_col)
-        def _(a=a):
-            o_ref[a] = jnp.zeros(o_ref.shape[1:], jnp.float32)
-
-    begin = jnp.logical_and(my_row == 1, my_col <= 1)
+        expected = jnp.where(jnp.logical_or(relayed, at(root_row, 1)), 3, 2)
+        for i, j in PASSED:
+            expected += jnp.where(at(*via(i, j)), 1, 0)
+        pl.semaphore_wait(barrier, expected)
+
+    tall = x_ref.shape[1]
+    corner_slot = steps + 1
+
+    def half_in(p):
+        span = pl.ds(p * (tall // 2), tall // 2)
+        return remote(x_ref.at[0, span], relay.at[2, span], half_sem.at[0, p], half_sem.at[1, p], (root_row, 1))
+
+    def half_on(p):
+        span = pl.ds(p * (tall // 2), tall // 2)
+        return remote(
+            relay.at[2, span], tiles.at[corner_slot, span], half_sem.at[2, p], in_sem.at[corner_slot], chief
+        )
+
+    begin = at(1, 0)
 
     @pl.when(begin)
     def _():
         to_chief(0).start()
+        to_chief(0).wait_send()
+
+    @pl.when(at(1, 1))
+    def _():
+        for p in range(2):
+            half_in(p).start()
+
+    @pl.when(at(root_row, 1))
+    def _():
+        for p in range(2):
+            half_in(p).wait_recv()
+            half_on(p).start()
+        signal(go_sem, (0, 1))
+
+    @pl.when(at(0, 1))
+    def _():
+        pl.semaphore_wait(go_sem, 1)
 
     early = jnp.logical_and(jnp.logical_and(my_row >= 2, my_row >= my_col), jnp.logical_not(is_helper))
 
@@ -250,16 +295,15 @@
     def _():
         to_relay(1).start()
 
-    for p in range(2):
+    for p in range(3):
 
         @pl.when(relays[p])
         def _(p=p):
             settle(relay.at[p], relay_in.at[p])
             onward(p).start()
 
-    last = num_row + my_row >= my_col
     late = jnp.logical_and(
-        last, jnp.logical_or(my_row == 2, jnp.logical_and(my_row < 2, jnp.logical_not(far)))
+        second, jnp.logical_or(jnp.logical_and(my_row == 2, my_col < 4), jnp.logical_and(my_row < 2, jnp.logical_not(far)))
     )
 
     @pl.when(late)
@@ -277,6 +321,10 @@
 
     def deliver(slot, a, row, col):
         return remote(tiles.at[slot], o_ref.at[a], out_sem.at[slot], land_sem.at[a], (row, col))
+
+    def hand(i, j):
+        slot = i * steps + j
+        return remote(tiles.at[slot], tiles.at[slot], out_sem.at[slot], in_sem.at[slot], via(i, j))
 
     def send(i, k):
         slot = i * steps + k
@@ -287,7 +335,16 @@
         def _():
             local(tiles.at[slot], o_ref.at[a], out_sem.at[slot]).start()
 
-        @pl.when(jnp.logical_not(home))
+        through = jnp.zeros((), jnp.bool_)
+        for p, q in PASSED:
+            here = jnp.logical_and(i == p, k == q)
+            through = jnp.logical_or(through, here)
+
+            @pl.when(here)
+            def _(p=p, q=q):
+                hand(p, q).start()
+
+        @pl.when(jnp.logical_not(jnp.logical_or(home, through)))
         def _():
             deliver(slot, a, row, k).start()
 
@@ -297,57 +354,89 @@
     def side_copy(k):
         return remote(tiles.at[(k + 1) * steps + k], beside.at[k], side_out.at[k], side_in.at[k], helper)
 
+    rows = lax.broadcasted_iota(jnp.int32, (width, width), 0)
+    cols = lax.broadcasted_iota(jnp.int32, (width, width), 1)
+
+    def scales():
+        only = jnp.where(rows == cols, work[...], 0.0)
+        along = jnp.sum(only, axis=0, keepdims=True)
+        down = jnp.sum(only, axis=1, keepdims=True)
+        return along, down, lax.rsqrt(along), lax.rsqrt(down)
+
+    def factor_of(along, down, scale_row, scale_col):
+        upper = jnp.where(cols // SUBS > rows // SUBS, work[...] * (along * scale_row), 0.0)
+        wide = jnp.concatenate([corner[...]] * (width // LANES), 1)
+        near = jnp.logical_and(cols // SUBS == rows // SUBS, cols <= rows)
+        return upper.T + jnp.where(near, wide * (down * scale_col), 0.0)
+
+    def first_part(start):
+        span = pl.ds(2 * start, 2 * PANEL)
+        return remote(
+            inverse.at[0, span], inverse.at[0, span], first_out.at[start // PANEL], first_in.at[start // PANEL], chief
+        )
+
+    first_waits = 3
+
     @pl.when(first)
     def _():
-        local(x_ref.at[0], tiles.at[0], in_sem.at[0]).start()
-
-    @pl.when(jnp.logical_or(first, is_chief))
+        work[...] = load(x_ref.at[0])
+        along, down, scale_row, scale_col = scales()
+        work[...] = work[...] * scale_row * scale_col
+        def after(start):
+            if start == 0:
+                pl.semaphore_wait(barrier, first_waits)
+            span = pl.ds(start, PANEL)
+            kept = jnp.where(cols[:PANEL] <= rows[:PANEL] + start, work[span, :], 0.0)
+            for h in range(width // LANES):
+                inverse[0, pl.ds(2 * start + h, PANEL, stride=2), :] = kept[:, h * LANES : (h + 1) * LANES]
+            first_part(start).start()
+
+        factor_tile(work, corner, scale_row, width, after)
+        to_relay(1).start()
+        store(o_ref.at[0], factor_of(along, down, scale_row, scale_col))
+        for start in range(0, width, PANEL):
+            first_part(start).wait_send()
+
+    @pl.when(is_chief)
     def _():
         def step(k, carry):
             slot = k * steps + k
 
-            @pl.when(is_chief)
-            def _():
-                @pl.when(k == 1)
-                def _():
-                    settle(inverse.at[0], inv_in.at[0])
-                    inv_high[0], inv_low[0] = split(load(inverse.at[0]))
-
-                left = slot - 1
-                arrive(left)
-                a_high, a_low = split(load(tiles.at[left]))
-                solved = dot3(a_high, a_low, inv_high[0], inv_low[0])
-                store(tiles.at[left], solved)
-                own_high[...], own_low[...] = split(solved)
-
-                @pl.when(k < steps - 1)
-                def _():
-                    side_copy(k - 1).start()
-
-                send(k, k - 1)
-
-            arrive(slot)
-
             @pl.when(k == 1)
             def _():
-                for p in range(2):
-                    for q in range(2, 4):
-                        signal(go_sem, (p, q))
+                for start in range(0, width, PANEL):
+                    first_part(start).wait_recv()
+                inv_copy(0, inv_out.at[0], helper).start()
+                for q in range(2, 4):
+                    signal(go_sem, (0, q))
+                inv_high[0], inv_low[0] = split(load(inverse.at[0]))
+
+            @pl.when(k == 2)
+            def _():
+                for q in range(2, 4):
+                    signal(go_sem, (1, q))
+
+            left = slot - 1
+            arrive(left)
+            a_high, a_low = split(load(tiles.at[left]))
+            solved = dot3(a_high, a_low, inv_high[0], inv_low[0])
+            store(tiles.at[left], solved)
+            own_high[...], own_low[...] = split(solved)
+
+            @pl.when(k < steps - 1)
+            def _():
+                side_copy(k - 1).start()
+
+            send(k, k - 1)
+
+            arrive(slot)
 
             work[...] = load(tiles.at[slot])
 
-            @pl.when(is_chief)
-            def _():
-                work[...] -= dot3(own_high[...], own_low[...], own_high[...], own_low[...])
-
-            rows = lax.broadcasted_iota(jnp.int32, (width, width), 0)
-            cols = lax.broadcasted_iota(jnp.int32, (width, width), 1)
-            tile = work[...]
-            only = jnp.where(rows == cols, tile, 0.0)
-            along = jnp.sum(only, axis=0, keepdims=True)
-            down = jnp.sum(only, axis=1, keepdims=True)
-            scale_row, scale_col = lax.rsqrt(along), lax.rsqrt(down)
-            work[...] = tile * scale_row * scale_col
+            work[...] -= dot3(own_high[...], own_low[...], own_high[...], own_low[...])
+
+            along, down, scale_row, scale_col = scales()
+            work[...] = work[...] * scale_row * scale_col
             factor_tile(work, corner, scale_row, width)
 
             @pl.when(k < steps - 1)
@@ -356,34 +445,16 @@
                 store(inverse.at[k], found)
                 inv_high[0], inv_low[0] = split(found)
 
-            @pl.when(first)
-            def _():
-                pl.semaphore_wait(barrier, 3)
-                inv_copy(k, first_out.at[0], chief).start()
-                inv_copy(k, first_out.at[1], helper).start()
-
-            @pl.when(jnp.logical_and(is_chief, k < steps - 2))
+            @pl.when(k < steps - 2)
             def _():
                 inv_copy(k, inv_out.at[k], helper).start()
 
-            upper = jnp.where(cols // SUBS > rows // SUBS, work[...] * (along * scale_row), 0.0)
-            wide = jnp.concatenate([corner[...]] * (width // LANES), 1)
-            near = jnp.logical_and(cols // SUBS == rows // SUBS, cols <= rows)
-            store(tiles.at[slot], upper.T + jnp.where(near, wide * (down * scale_col), 0.0))
+            store(tiles.at[slot], factor_of(along, down, scale_row, scale_col))
             send(k, k)
             return carry
 
-        lax.fori_loop(jnp.where(first, 0, 1), jnp.where(first, 1, steps), step, 0)
-
-    @pl.when(first)
-    def _():
-        to_relay(1).start()
-        settle(tiles.at[0], out_sem.at[0])
-        inv_copy(0, first_out.at[0], chief).wait_send()
-        inv_copy(0, first_out.at[1], helper).wait_send()
-
-    @pl.when(is_chief)
-    def _():
+        lax.fori_loop(1, steps, step, 0)
+
         def finish(k, carry):
             settle(tiles.at[k * steps + k], out_sem.at[k * steps + k])
             settle(tiles.at[k * steps + k - 1], out_sem.at[k * steps + k - 1])
@@ -399,6 +470,7 @@
             return carry
 
         lax.fori_loop(1, steps, finish, 0)
+        settle(inverse.at[0], inv_out.at[0])
 
     def block(i):
         return pl.ds(pl.multiple_of(i * width, width), width)
@@ -414,7 +486,7 @@
 
             @pl.when(i == 2)
             def _():
-                for q in range(num_col - 1):
+                for q in range(4):
                     signal(go_sem, (2, q))
 
             def stage(k, carry):
@@ -432,16 +504,27 @@
                 high[block(i), block(k)], low[block(i), block(k)] = split(solved)
                 send(i, k)
 
-                def one(j, carry):
-                    slot = i * steps + j
+                def some(j, size):
+                    span = pl.ds(pl.multiple_of(j * width, width), size * width)
                     update = dot3(
-                        high[block(i), block(k)], low[block(i), block(k)],
-                        high[block(j), block(k)], low[block(j), block(k)],
+                        high[block(i), block(k)], low[block(i), block(k)], high[span, block(k)], low[span, block(k)]
                     )
-                    store(tiles.at[slot], load(tiles.at[slot]) - update)
+                    for t in range(size):
+                        slot = i * steps + j + t
+                        part = update[:, t * width : (t + 1) * width]
+                        store(tiles.at[slot], load(tiles.at[slot]) - part)
+
+                def three(q, carry):
+                    some(k + 1 + 3 * q, 3)
                     return carry
 
-                lax.fori_loop(k + 1, i + 1, one, 0)
+                lax.fori_loop(0, (i - k) // 3, three, 0)
+                for rest in (1, 2):
+
+                    @pl.when(lax.rem(i - k, 3) == rest)
+                    def _(rest=rest):
+                        some(i + 1 - rest, rest)
+
                 return carry
 
             lax.fori_loop(0, i - 1, stage, 0)
@@ -464,7 +547,33 @@
 
         lax.fori_loop(2, steps, finish, 0)
 
-    sent = [jnp.logical_or(begin, early), jnp.logical_or(relayed, end)]
+    def onto(i, j):
+        return deliver(i * steps + j, i // num_row, i % num_row, j)
+
+    for i, j in PASSED:
+
+        @pl.when(at(*via(i, j)))
+        def _(i=i, j=j):
+            arrive(i * steps + j)
+            onto(i, j).start()
+
+    for i, j in PASSED:
+
+        @pl.when(at(*via(i, j)))
+        def _(i=i, j=j):
+            onto(i, j).wait_send()
+
+    @pl.when(at(1, 1))
+    def _():
+        for p in range(2):
+            half_in(p).wait_send()
+
+    @pl.when(at(root_row, 1))
+    def _():
+        for p in range(2):
+            half_on(p).wait_send()
+
+    sent = [early, jnp.logical_or(relayed, end)]
     for a in range(row_tiles):
 
         @pl.when(sent[a])
@@ -480,7 +589,7 @@
         def _(a=a):
             settle(o_ref.at[a], land_sem.at[a])
 
-    for p in range(2):
+    for p in range(3):
 
         @pl.when(relays[p])
         def _(p=p):
@@ -505,7 +614,7 @@
             pltpu.VMEM((slots, tall, LANES), jnp.float32),
             pltpu.VMEM((STEPS, tall, LANES), jnp.float32),
             pltpu.VMEM((STEPS, tall, LANES), jnp.float32),
-            pltpu.VMEM((2, tall, LANES), jnp.float32),
+            pltpu.VMEM((3, tall, LANES), jnp.float32),
             pltpu.VMEM((order, order), jnp.bfloat16),
             pltpu.VMEM((order, order), jnp.bfloat16),
             pltpu.VMEM((width, width), jnp.bfloat16),
@@ -514,13 +623,17 @@
             pltpu.VMEM((STEPS, width, width), jnp.bfloat16),
             pltpu.VMEM((width, width), jnp.float32),
             pltpu.VMEM((width, LANES), jnp.float32),
-            sem((slots,)), sem((slots,)), sem((slots,)), sem((STEPS,)), sem((STEPS,)), sem((2,)), sem((STEPS,)),
-            sem((STEPS,)), sem((row_tiles,)), sem((row_tiles,)), sem((2,)), sem((2,)),
+            sem((slots,)), sem((slots,)), sem((slots,)), sem((STEPS,)), sem((STEPS,)),
+            sem((width // PANEL,)), sem((width // PANEL,)), sem((STEPS,)),
+            sem((STEPS,)), sem((row_tiles,)), sem((row_tiles,)), sem((3,)), sem((3,)),
+            sem((3, 2)),
             pltpu.SemaphoreType.REGULAR,
         ],
         compiler_params=pltpu.CompilerParams(collective_id=0, has_side_effects=True, vmem_limit_bytes=56 * 2**20),
     )(local)
-    return out.reshape(matrix.shape)
+    rows = jnp.arange(row_tiles) * num_row + lax.axis_index("row")
+    kept = jnp.where((rows >= lax.axis_index("col"))[:, None, None], out, 0.0)
+    return kept.reshape(matrix.shape)
 
 
 def broadcast(value, axis, source):

time: 73.3 us -> 64 us (0.87)
  Pallas kernels: 70.9 us -> 61.8 us
  local copies, waits for them, and re-layouts: 2.19 us -> 0 us
  other arithmetic: 0 us -> 1.95 us
    pallas_call x1, Pallas kernels: 70.9 us -> 61.8 us  [on_root(): pl.pallas_call(functools.partial(kernel, (STEPS, num_row, num_col)), out_...]
    unnamed x1 -> x0, local copies, waits for them, and re-layouts: 2.19 us -> none
    select_n x0 -> x1, other arithmetic: none -> 1.94 us  [on_root(): kept = jnp.where((rows >= lax.axis_index('col'))[:, None, None], out, 0.0)]
where the time goes in v3:
time: 64 us; the launch traced here: 63.8 us
  Pallas kernels  61.8 us (97%)
  other arithmetic  1.95 us (3%)
    pallas_call x1, Pallas kernels, on_root(): pl.pallas_call(functools.partial(kernel, (STEPS, num_row, num_col)), out_...  61.8 us
    select_n x1, other arithmetic, on_root(): kept = jnp.where((rows >= lax.axis_index('col'))[:, None, None], out, 0.0)  1.94 us

profile of v3, /device:TPU:31, one launch (start us, length us, event | category | flops | bytes accessed | tf_op | source)
XLA Modules:
  0.0 63.8 jit_solution(12610506265241169320)
XLA Ops:
  0.0 61.8 %shard_map.17 = f32[2,512,128]{2,1,0:T(8,128)} custom-call(f32[2,512,128]{2,1,0:T(8,128)} %bitcast.2), custom_call_target="tpu_custom_call" | custom-call | tf_op jit(solution)/shard_map/pallas_call | solution.py:608
  61.9 1.9 %broadcast_select_fusion = f32[2,512,128]{2,1,0:T(8,128)} fusion(f32[2,512,128]{2,1,0:T(8,128)} %shard_map.17, pred[2]{0:T(512)(128)(4,1)S(1)} %add_compare_fusion), kind=kLoop, calls=%fused_computation | loop fusion | flops 131072 | bytes 1048578 | tf_op jit(solution)/shard_map/jit(_where)/select_n | solution.py:635
  (1 shorter events, 0.0 us)

commit v4 on v3

--- a/solution.py
+++ b/solution.py
@@ -48,7 +48,7 @@
         hc, off = l0//LANES, l0%LANES
         def pick(g, t):
             return jnp.take_along_axis(rows[g][hc], jnp.full(SHAPE, off+t, jnp.int32), axis=1)
-        near = min(home+2*per, groups)
+        near = min(home+per, groups)
         far = list(range(near, groups))
         cols = [{g: pick(g,t) for g in range(home + t//SUBS, near)} for t in range(BLOCK)]
         fcols = [{g: pick(g,t) for g in far} for t in range(SUBS)] + [{}]*SUBS
@@ -514,14 +514,14 @@
                         part = update[:, t * width : (t + 1) * width]
                         store(tiles.at[slot], load(tiles.at[slot]) - part)
 
-                def three(q, carry):
-                    some(k + 1 + 3 * q, 3)
+                def four(q, carry):
+                    some(k + 1 + 4 * q, 4)
                     return carry
 
-                lax.fori_loop(0, (i - k) // 3, three, 0)
-                for rest in (1, 2):
-
-                    @pl.when(lax.rem(i - k, 3) == rest)
+                lax.fori_loop(0, (i - k) // 4, four, 0)
+                for rest in (1, 2, 3):
+
+                    @pl.when(lax.rem(i - k, 4) == rest)
                     def _(rest=rest):
                         some(i + 1 - rest, rest)
 

time: 64 us -> 63.4 us (level)
  no operation moved by 1% of the time
where the time goes in v4:
time: 63.4 us; the launch traced here: 63.2 us
  Pallas kernels  61.2 us (97%)
  other arithmetic  1.95 us (3%)
    pallas_call x1, Pallas kernels, on_root(): pl.pallas_call(functools.partial(kernel, (STEPS, num_row, num_col)), out_...  61.2 us
    select_n x1, other arithmetic, on_root(): kept = jnp.where((rows >= lax.axis_index('col'))[:, None, None], out, 0.0)  1.94 us

profile of v4, /device:TPU:31, one launch (start us, length us, event | category | flops | bytes accessed | tf_op | source)
XLA Modules:
  0.0 63.2 jit_solution(2948440555769863106)
XLA Ops:
  0.0 61.2 %shard_map.17 = f32[2,512,128]{2,1,0:T(8,128)} custom-call(f32[2,512,128]{2,1,0:T(8,128)} %bitcast.2), custom_call_target="tpu_custom_call" | custom-call | tf_op jit(solution)/shard_map/pallas_call | solution.py:608
  61.3 1.9 %broadcast_select_fusion = f32[2,512,128]{2,1,0:T(8,128)} fusion(f32[2,512,128]{2,1,0:T(8,128)} %shard_map.17, pred[2]{0:T(512)(128)(4,1)S(1)} %add_compare_fusion), kind=kLoop, calls=%fused_computation | loop fusion | flops 131072 | bytes 1048578 | tf_op jit(solution)/shard_map/jit(_where)/select_n | solution.py:635
  (1 shorter events, 0.0 us)
